TPU v7x, 32 devices: a whole 2x2x4 slice. The times are simulated.
32 devices in a mesh: wide: 16 (over z, y, x), narrow: 2 (over core).
Axes of the slice: x: 2, y: 2, z: 4, core: 2. Of those that a mesh axis runs over, the one named last changes fastest.
Arguments:
- tokens: bfloat16 [2048, 2048], P('wide'), may hold values from -6 to 6
- expert_ids: int32 [2048, 6], P('wide'), may hold values from 0 to 15, all different within a row; in each aligned block of 128 rows (0 to 127, 128 to 255, ...) at most 64 rows name the same one
- gate_weights: float32 [2048, 6], P('wide'), may hold values from 0.05 to 0.6
- shared_gate: bfloat16 [2048, 2816], P('wide', 'narrow'), may hold values from -0.125 to 0.125
- shared_up: bfloat16 [2048, 2816], P('wide', 'narrow'), may hold values from -0.125 to 0.125
- shared_down: bfloat16 [2816, 2048], P('narrow', 'wide'), may hold values from -0.109375 to 0.109375
- expert_gate: bfloat16 [16, 2048, 1408], P('wide', None, 'narrow'), may hold values from -0.125 to 0.125
- expert_up: bfloat16 [16, 2048, 1408], P('wide', None, 'narrow'), may hold values from -0.125 to 0.125
- expert_down: bfloat16 [16, 1408, 2048], P('wide', 'narrow'), may hold values from -0.15625 to 0.15625
Outputs:
- moe_out: bfloat16 [2048, 2048], P('wide', 'narrow')
Inputs may be any that keep to these rules, and one draw needn't show every extreme that they name: `expert_ids`: the 6 ids of a row differ. Among the 128 rows of one index of wide, no expert is named by more than 64 rows.
All inputs are finite; a program needn't handle non-finite values.
Results may differ from a plain program's by a relative error of at most 0.0075.
Values may be sent and summed in bfloat16 or wider, within the bound.
A program may use at most 128 MiB of HBM per device.

v0:
```python
import jax
import jax.numpy as jnp
from jax import lax
from jax.sharding import PartitionSpec as P


def expert_ffn(received, w_gate, w_up, w_down):
    senders, items, width = received.shape
    flat_rows = received.reshape(senders * items, width)
    gate_part = jnp.dot(flat_rows, w_gate, preferred_element_type=jnp.float32)
    up_part = jnp.dot(flat_rows, w_up, preferred_element_type=jnp.float32)
    hidden = (jax.nn.silu(gate_part) * up_part).astype(jnp.bfloat16)
    partial_value = jnp.dot(hidden, w_down, preferred_element_type=jnp.float32).astype(jnp.bfloat16)
    return partial_value.reshape(senders, items, w_down.shape[1])


def body(
    tokens,
    expert_ids,
    gate_weights,
    shared_gate,
    shared_up,
    shared_down,
    expert_gate,
    expert_up,
    expert_down,
):
    tok_count, width = tokens.shape
    top_count = expert_ids.shape[1]
    experts = lax.axis_size("wide") * expert_gate.shape[0]
    capacity = min(tok_count, 4 * tok_count * top_count // (3 * experts))
    narrow_count = lax.axis_size("narrow")
    w_gate = expert_gate[0]
    w_up = expert_up[0]
    w_down = expert_down[0]
    pairs = tok_count * top_count
    flat_ids = expert_ids.reshape(pairs)
    onehot = (flat_ids[:, None] == jnp.arange(experts, dtype=jnp.int32)[None, :]).astype(jnp.int32)
    before = jnp.cumsum(onehot, axis=0) - onehot
    slot_pos = jnp.sum(before * onehot, axis=1)
    target_slot = flat_ids * capacity + slot_pos
    source = (
        jnp.full((experts * capacity,), -1, jnp.int32)
        .at[target_slot]
        .set(jnp.arange(pairs, dtype=jnp.int32))
    )
    filled = source >= 0
    token_of = jnp.where(filled, source // top_count, 0)
    outgoing = jnp.where(filled[:, None], tokens[token_of], jnp.zeros((), jnp.bfloat16))
    outgoing = outgoing.reshape(experts, capacity, width)
    quarter = capacity // narrow_count
    own_rows = lax.dynamic_slice_in_dim(outgoing, lax.axis_index("narrow") * quarter, quarter, 1)
    arrived = lax.all_to_all(own_rows, "wide", split_axis=0, concat_axis=0, tiled=True)
    joined = lax.all_gather(arrived, "narrow", axis=1, tiled=True)
    partial_value = expert_ffn(joined, w_gate, w_up, w_down)
    expert_out = (
        lax.psum_scatter(partial_value, "narrow", scatter_dimension=2, tiled=True)
        .astype(jnp.float32)
        .astype(jnp.bfloat16)
    )
    returned = lax.all_to_all(expert_out, "wide", split_axis=0, concat_axis=0, tiled=True)
    returned_rows = returned.reshape(experts * capacity, returned.shape[2])
    pair_rows = returned_rows[target_slot].astype(jnp.float32)
    weighted = gate_weights.reshape(pairs, 1) * pair_rows
    routed = jnp.sum(weighted.reshape(tok_count, top_count, returned.shape[2]), axis=1)
    gate_sum = jnp.dot(
        tokens,
        lax.all_gather(shared_gate, "wide", axis=0, tiled=True),
        preferred_element_type=jnp.float32,
    )
    up_sum = jnp.dot(
        tokens,
        lax.all_gather(shared_up, "wide", axis=0, tiled=True),
        preferred_element_type=jnp.float32,
    )
    shared_hidden = (jax.nn.silu(gate_sum) * up_sum).astype(jnp.bfloat16)
    shared_terms = jnp.dot(
        shared_hidden,
        lax.all_gather(shared_down, "wide", axis=1, tiled=True),
        preferred_element_type=jnp.float32,
    )
    shared = lax.psum_scatter(shared_terms, "narrow", scatter_dimension=1, tiled=True)
    return (shared + routed).astype(jnp.bfloat16)


def solution(mesh):
    in_specs = (
        P("wide", None),
        P("wide", None),
        P("wide", None),
        P("wide", "narrow"),
        P("wide", "narrow"),
        P("narrow", "wide"),
        P("wide", None, "narrow"),
        P("wide", None, "narrow"),
        P("wide", "narrow", None),
    )
    out_specs = P("wide", "narrow")
    return jax.shard_map(body, mesh=mesh, in_specs=in_specs, out_specs=out_specs, check_vma=False)
```

profile of v0, /device:TPU:0, one launch (start us, length us, event | category | flops | bytes accessed | tf_op | source)
XLA Modules:
  0.0 462.6 jit_solution(8130816217768334769)
XLA Ops:
  7.4 0.0 copy-start
  7.4 0.0 all-gather.11.cloned.1.call-start
  7.4 0.8 broadcast_multiply_fusion
  8.2 0.9 copy.13
  9.1 0.1 eq.29
  9.3 0.1 eq.25
  9.4 0.1 copy.12
  9.5 0.1 mul.50
  9.7 1.7 reduce-window.6
  11.4 0.3 slice_reduce_fusion
  11.7 0.1 fusion.14
  11.8 3.4 scatter_custom_fusion
  15.2 0.1 broadcast_in_dim.27
  15.3 0.1 constant_dynamic-slice_fusion
  15.4 0.0 copy-done.1
  15.4 6.0 %gather_fusion = bf16[1024,2048]{1,0:T(8,128)(2,1)} fusion(bf16[128,2048]{1,0:T(8,128)(2,1)S(1)} %copy-done.1, s32[1024]{0:T(1024)S(1)} %fusion.17), kind=kCustom, calls=%fused_computation | custom fusion | bytes 8392704 | tf_op jit(solution)/shard_map/gather | solution.py:49
  21.4 2.0 dynamic-slice_select_fusion
  23.4 57.0 %all_to_all.10 = bf16[16,32,2048]{2,1,0:T(8,128)(2,1)} all-to-all(bf16[16,32,2048]{2,1,0:T(8,128)(2,1)S(1)} %dynamic-slice_select_fusion), channel_id=1, replica_groups=mesh['wide'=16,'narrow'=2] {'wide'}, dimensions={0} | all-to-all | bytes 4194304 | tf_op jit(solution)/shard_map/all_to_all | solution.py:53
  80.5 0.0 all-gather.11.cloned.1.call-update
  80.5 0.0 reduce-scatter.5.cloned.1.call-start
  80.5 12.1 %all-gather.11.cloned.1.call-done = bf16[16,64,2048]{2,1,0:T(8,128)(2,1)} async-done(((bf16[16,32,2048]{2,1,0:T(8,128)(2,1)}), bf16[16,64,2048]{2,1,0:T(8,128)(2,1)}) %all-gather.11.cloned.1.call-update) | async-done | bytes 4194320 | tf_op jit(solution)/shard_map/all_gather | solution.py:54
  92.6 7.9 %fusion.1 = f32[1024,704]{0,1:T(8,128)} fusion(bf16[1024,2048]{1,0:T(8,128)(2,1)} %bitcast.48, bf16[1,2048,704]{1,2,0:T(8,128)(2,1)} %param.16), kind=kOutput, calls=%fused_computation.6 | convolution fusion | flops 2952790016 | bytes 9961472 | tf_op jit(solution)/shard_map/dot_general | solution.py:11
  100.5 0.0 copy-done
  100.5 11.3 %convolution_convert_fusion = bf16[1024,2048]{1,0:T(8,128)(2,1)} fusion(bf16[1,704,2048]{2,1,0:T(8,128)(2,1)S(1)} %copy-done, f32[1024,704]{0,1:T(8,128)} %fusion.1, bf16[1024,2048]{1,0:T(8,128)(2,1)} %bitcast.49, bf16[1,2048,704]{1,2,0:T(8,128)(2,1)} %param.15), kind=kOutput, calls=%fused_computation.4 | convolution fusion | flops 5912002560 | bytes 17039360 | tf_op jit(solution)/shard_map/dot_general | solution.py:13
  111.8 0.0 reduce-scatter.5.cloned.1.call-update
  111.8 0.0 all-gather.5.cloned.1.call-start
  111.9 0.5 all-gather.5.cloned.1.call-update
  112.4 0.0 all-gather.7.cloned.1.call-start
  112.4 0.5 all-gather.7.cloned.1.call-update
  113.0 0.0 all-gather.9.cloned.1.call-start
  113.0 0.5 all-gather.9.cloned.1.call-update
  113.6 11.5 %reduce-scatter.5.cloned.1.call-done = bf16[16,64,1024]{2,1,0:T(8,128)(2,1)} async-done(((bf16[16,64,2048]{2,1,0:T(8,128)(2,1)}), bf16[16,64,1024]{2,1,0:T(8,128)(2,1)}) %reduce-scatter.5.cloned.1.call-update) | async-done | bytes 2097168 | tf_op jit(solution)/shard_map/reduce_scatter | solution.py:57
  125.0 7.0 %all-to-all-start.1 = ((bf16[16,64,1024]{2,1,0:T(8,128)(2,1)}), bf16[16,64,1024]{2,1,0:T(8,128)(2,1)}, u32[]{:S(2)}, u32[]{:S(2)}) async-start(bf16[16,64,1024]{2,1,0:T(8,128)(2,1)} %reduce-scatter.5.cloned.1.call-done), calls=%async_computation.3 | async-start | bytes 4194304 | tf_op jit(solution)/shard_map/all_to_all | solution.py:61
  132.0 0.2 reduce-scatter.3.cloned.1.call-start
  132.2 100.1 %all-gather.5.cloned.1.call-done = bf16[2048,1408]{1,0:T(8,128)(2,1)} async-done(((bf16[128,1408]{1,0:T(8,128)(2,1)}), bf16[2048,1408]{1,0:T(8,128)(2,1)}) %all-gather.5.cloned.1.call-update) | async-done | bytes 5767184 | tf_op jit(solution)/shard_map/all_gather | solution.py:68
  232.3 4.5 fusion.24
  236.8 85.5 %all-gather.7.cloned.1.call-done = bf16[2048,1408]{1,0:T(8,128)(2,1)} async-done(((bf16[128,1408]{1,0:T(8,128)(2,1)}), bf16[2048,1408]{1,0:T(8,128)(2,1)}) %all-gather.7.cloned.1.call-update) | async-done | bytes 5767184 | tf_op jit(solution)/shard_map/all_gather | solution.py:73
  322.4 109.5 %all-gather.9.cloned.1.call-done = bf16[1408,2048]{1,0:T(8,128)(2,1)} async-done(((bf16[1408,128]{1,0:T(8,128)(2,1)}), bf16[1408,2048]{1,0:T(8,128)(2,1)}) %all-gather.9.cloned.1.call-update) | async-done | bytes 5767184 | tf_op jit(solution)/shard_map/all_gather | solution.py:79
  431.9 7.5 %fusion.10 = f32[128,2048]{1,0:T(8,128)} fusion(bf16[1408,2048]{1,0:T(8,128)(2,1)} %all-gather.9.cloned.1.call-done, bf16[128,2048]{1,0:T(8,128)(2,1)S(1)} %copy-done.1, bf16[2048,1408]{1,0:T(8,128)(2,1)} %all-gather.7.cloned.1.call-done, f32[128,1408]{1,0:T(8,128)} %fusion.24), kind=kOutput, calls=%fused_computation.14 | convolution fusion | flops 1477476352 | bytes 13828096 | tf_op jit(solution)/shard_map/dot_general | solution.py:77
  439.3 0.0 reduce-scatter.3.cloned.1.call-update
  439.4 0.0 copy-done.2
  439.4 0.1 copy.11
  439.5 0.0 all-to-all-done.1
  439.5 6.4 %gather_fusion.1 = bf16[768,1024]{1,0:T(8,128)(2,1)} fusion(bf16[1024,1024]{1,0:T(8,128)(2,1)} %bitcast.7, s32[1024]{0:T(1024)S(1)} %pad_clamp_fusion), kind=kCustom, calls=%fused_computation.1 | custom fusion | bytes 3148800 | tf_op jit(solution)/shard_map/gather | solution.py:63
  445.9 3.9 reshape.78
  449.8 3.6 multiply_reduce_fusion
  453.4 0.0 reduce-scatter.3.cloned.1.call-done
  453.4 1.8 add_convert_fusion
  (9 shorter events, 0.1 us)
Async XLA Ops:
  7.4 93.1 %copy-start = (bf16[1,704,2048]{2,1,0:T(8,128)(2,1)S(1)}, bf16[1,704,2048]{2,1,0:T(8,128)(2,1)}, u32[]{:S(2)}) copy-start(bf16[1,704,2048]{2,1,0:T(8,128)(2,1)} %param.17) | copy-start | bytes 8650756
  7.4 8.0 %copy-start.1 = (bf16[128,2048]{1,0:T(8,128)(2,1)S(1)}, bf16[128,2048]{1,0:T(8,128)(2,1)}, u32[]{:S(2)}) copy-start(bf16[128,2048]{1,0:T(8,128)(2,1)} %param.9) | copy-start | bytes 1572868
  7.4 85.3 %all-gather.11.cloned.1.call-start = ((), (), s32[]{:S(2)}) async-start(), calls=%async_computation.8 | async-start | bytes 6291456 | tf_op jit(solution)/shard_map/all_gather | solution.py:54
  80.5 44.5 %reduce-scatter.5.cloned.1.call-start = ((), (), s32[]{:S(2)}) async-start(), calls=%async_computation.9 | async-start | bytes 6291456 | tf_op jit(solution)/shard_map/reduce_scatter | solution.py:57
  111.8 120.5 %all-gather.5.cloned.1.call-start = ((), (), s32[]{:S(2)}) async-start(), calls=%async_computation.4 | async-start | bytes 6127616 | tf_op jit(solution)/shard_map/all_gather | solution.py:68
  112.4 210.0 %all-gather.7.cloned.1.call-start = ((), (), s32[]{:S(2)}) async-start(), calls=%async_computation.5 | async-start | bytes 6127616 | tf_op jit(solution)/shard_map/all_gather | solution.py:73
  113.0 318.9 %all-gather.9.cloned.1.call-start = ((), (), s32[]{:S(2)}) async-start(), calls=%async_computation.6 | async-start | bytes 6127616 | tf_op jit(solution)/shard_map/all_gather | solution.py:79
  125.0 314.5 %all-to-all-start.1 = ((bf16[16,64,1024]{2,1,0:T(8,128)(2,1)}), bf16[16,64,1024]{2,1,0:T(8,128)(2,1)}, u32[]{:S(2)}, u32[]{:S(2)}) async-start(bf16[16,64,1024]{2,1,0:T(8,128)(2,1)} %reduce-scatter.5.cloned.1.call-done), calls=%async_computation.3 | async-start | bytes 4194304 | tf_op jit(solution)/shard_map/all_to_all | solution.py:61
  132.0 321.4 %reduce-scatter.3.cloned.1.call-start = ((), (), s32[]{:S(2)}) async-start(), calls=%async_computation.7 | async-start | bytes 1572864 | tf_op jit(solution)/shard_map/reduce_scatter | solution.py:82
  236.8 202.5 %copy-start.2 = (f32[128,6]{0,1:T(8,128)S(1)}, f32[128,6]{0,1:T(8,128)}, u32[]{:S(2)}) copy-start(f32[128,6]{0,1:T(8,128)} %param.11) | copy-start | bytes 9220
Sparse Core Ops, SparseCore 0:
  80.6 11.9 all-gather.10
  111.9 13.0 reduce-scatter.4
  439.5 6.5 reduce-scatter.2
Sparse Core Ops, SparseCore 1:
  115.0 117.3 all-gather.4
  234.9 87.4 all-gather.6
  324.9 106.9 all-gather.8
where the time goes:
time: 463 us
  waiting for transfers between devices  320 us (69%)
  blocking collectives  57 us (12%)
  matrix products  31.1 us (7%)
  local copies, waits for them, and re-layouts  21.7 us (5%)
  between operations  14.9 us (3%)
  other arithmetic  10.1 us (2%)
  starting transfers between devices  7.34 us (2%)
    all_gather x1, waiting for transfers between devices, body(): lax.all_gather(shared_down, 'wide', axis=1, tiled=True)  110 us
    all_gather x1, waiting for transfers between devices, body(): lax.all_gather(shared_gate, 'wide', axis=0, tiled=True)  100 us
    all_gather x1, waiting for transfers between devices, body(): lax.all_gather(shared_up, 'wide', axis=0, tiled=True)  85.5 us
    all_to_all x1, blocking collectives, body(): lax.all_to_all(own_rows, 'wide', split_axis=0, concat_axis=0, tiled=True)  57 us
    all_gather x1, waiting for transfers between devices, body(): joined = lax.all_gather(arrived, 'narrow', axis=1, tiled=True)  12.1 us
    reduce_scatter x1, waiting for transfers between devices, body(): lax.psum_scatter(partial_value, 'narrow', scatter_dimension=2, tiled=True)  11.5 us
    dot_general x1, matrix products, expert_ffn(): jnp.dot(hidden, w_down, preferred_element_type=jnp.float32)  11.3 us
  transfers between devices with their start and end apart: 7, of which 5 were waited for; matrix products, arithmetic and copies ran while one was open for 6% of the time, Pallas kernels for 0%

commit v1 on v0

--- a/solution.py
+++ b/solution.py
@@ -2,6 +2,12 @@
 import jax.numpy as jnp
 from jax import lax
 from jax.sharding import PartitionSpec as P
+
+
+def stack_and_merge(array, axis, dim):
+    shards = lax.all_gather(array, axis, axis=0, tiled=False)
+    full = jnp.concatenate(shards, axis=dim)
+    return full
 
 
 def expert_ffn(received, w_gate, w_up, w_down):
@@ -75,9 +81,7 @@
     )
     shared_hidden = (jax.nn.silu(gate_sum) * up_sum).astype(jnp.bfloat16)
     shared_terms = jnp.dot(
-        shared_hidden,
-        lax.all_gather(shared_down, "wide", axis=1, tiled=True),
-        preferred_element_type=jnp.float32,
+        shared_hidden, stack_and_merge(shared_down, "wide", 1), preferred_element_type=jnp.float32
     )
     shared = lax.psum_scatter(shared_terms, "narrow", scatter_dimension=1, tiled=True)
     return (shared + routed).astype(jnp.bfloat16)

time: 463 us -> 444 us (0.959)
  waiting for transfers between devices: 320 us -> 292 us
  local copies, waits for them, and re-layouts: 21.7 us -> 30 us
    all_gather x1, waiting for transfers between devices: 100 us -> 81.8 us  [body(): lax.all_gather(shared_gate, 'wide', axis=0, tiled=True)]
    all_gather x1, waiting for transfers between devices: 110 us -> 100 us  [stack_and_merge(): shards = lax.all_gather(array, axis, axis=0, tiled=False)]
    reshape x0 -> x1, local copies, waits for them, and re-layouts: none -> 8.27 us  [stack_and_merge(): full = jnp.concatenate(shards, axis=dim)]
  transfers between devices with their start and end apart: 7 -> 7, of which waited for: 5 -> 5; matrix products, arithmetic and copies ran while one was open for 6% -> 8% of each run, Pallas kernels for 0% -> 0%
where the time goes in v1:
time: 444 us
  waiting for transfers between devices  292 us (66%)
  blocking collectives  57 us (13%)
  matrix products  32.1 us (7%)
  local copies, waits for them, and re-layouts  30 us (7%)
  between operations  14.9 us (3%)
  other arithmetic  9.95 us (2%)
  starting transfers between devices  7.34 us (2%)
    all_gather x1, waiting for transfers between devices, stack_and_merge(): shards = lax.all_gather(array, axis, axis=0, tiled=False)  100 us
    all_gather x1, waiting for transfers between devices, body(): lax.all_gather(shared_up, 'wide', axis=0, tiled=True)  85.3 us
    all_gather x1, waiting for transfers between devices, body(): lax.all_gather(shared_gate, 'wide', axis=0, tiled=True)  81.8 us
    all_to_all x1, blocking collectives, body(): lax.all_to_all(own_rows, 'wide', split_axis=0, concat_axis=0, tiled=True)  57 us
    all_gather x1, waiting for transfers between devices, body(): joined = lax.all_gather(arrived, 'narrow', axis=1, tiled=True)  12.1 us
    reduce_scatter x1, waiting for transfers between devices, body(): lax.psum_scatter(partial_value, 'narrow', scatter_dimension=2, tiled=True)  11.5 us
    dot_general x1, matrix products, expert_ffn(): jnp.dot(hidden, w_down, preferred_element_type=jnp.float32)  11.3 us
  transfers between devices with their start and end apart: 7, of which 5 were waited for; matrix products, arithmetic and copies ran while one was open for 8% of the time, Pallas kernels for 0%

profile of v1, /device:TPU:0, one launch (start us, length us, event | category | flops | bytes accessed | tf_op | source)
XLA Modules:
  0.0 443.7 jit_solution(6879990294401076113)
XLA Ops:
  7.4 0.0 copy-start
  7.4 0.0 all-gather.10.cloned.1.call-start
  7.4 0.9 copy.19
  8.3 0.1 eq.29
  8.5 0.1 eq.25
  8.6 0.7 broadcast_multiply_fusion
  9.3 1.7 reduce-window.6
  11.0 0.3 slice_reduce_fusion
  11.3 0.1 copy.18
  11.4 0.1 mul.50
  11.6 0.1 fusion.14
  11.7 3.4 scatter_custom_fusion
  15.1 0.1 broadcast_in_dim.27
  15.2 0.1 constant_dynamic-slice_fusion
  15.3 0.0 copy-done.1
  15.3 6.0 %gather_fusion = bf16[1024,2048]{1,0:T(8,128)(2,1)} fusion(bf16[128,2048]{1,0:T(8,128)(2,1)S(1)} %copy-done.1, s32[1024]{0:T(1024)S(1)} %fusion.17), kind=kCustom, calls=%fused_computation | custom fusion | bytes 8392704 | tf_op jit(solution)/shard_map/gather | solution.py:55
  21.3 2.0 dynamic-slice_select_fusion
  23.3 57.0 %all_to_all.10 = bf16[16,32,2048]{2,1,0:T(8,128)(2,1)} all-to-all(bf16[16,32,2048]{2,1,0:T(8,128)(2,1)S(1)} %dynamic-slice_select_fusion), channel_id=1, replica_groups=mesh['wide'=16,'narrow'=2] {'wide'}, dimensions={0} | all-to-all | bytes 4194304 | tf_op jit(solution)/shard_map/all_to_all | solution.py:59
  80.3 0.0 all-gather.10.cloned.1.call-update
  80.4 0.0 reduce-scatter.5.cloned.1.call-start
  80.4 12.1 %all-gather.10.cloned.1.call-done = bf16[16,64,2048]{2,1,0:T(8,128)(2,1)} async-done(((bf16[16,32,2048]{2,1,0:T(8,128)(2,1)}), bf16[16,64,2048]{2,1,0:T(8,128)(2,1)}) %all-gather.10.cloned.1.call-update) | async-done | bytes 4194320 | tf_op jit(solution)/shard_map/all_gather | solution.py:60
  92.5 7.9 %fusion.1 = f32[1024,704]{0,1:T(8,128)} fusion(bf16[1024,2048]{1,0:T(8,128)(2,1)} %bitcast.53, bf16[1,2048,704]{1,2,0:T(8,128)(2,1)} %param.16), kind=kOutput, calls=%fused_computation.6 | convolution fusion | flops 2952790016 | bytes 9961472 | tf_op jit(solution)/shard_map/dot_general | solution.py:17
  100.4 0.0 copy-done
  100.4 11.3 %convolution_convert_fusion = bf16[1024,2048]{1,0:T(8,128)(2,1)} fusion(bf16[1,704,2048]{2,1,0:T(8,128)(2,1)S(1)} %copy-done, f32[1024,704]{0,1:T(8,128)} %fusion.1, bf16[1024,2048]{1,0:T(8,128)(2,1)} %bitcast.54, bf16[1,2048,704]{1,2,0:T(8,128)(2,1)} %param.15), kind=kOutput, calls=%fused_computation.4 | convolution fusion | flops 5912002560 | bytes 17039360 | tf_op jit(solution)/shard_map/dot_general | solution.py:19
  111.7 0.0 reduce-scatter.5.cloned.1.call-update
  111.7 0.0 all-gather.12.cloned.1.call-start
  111.7 0.5 all-gather.12.cloned.1.call-update
  112.3 0.0 all-gather.6.cloned.1.call-start
  112.3 0.5 all-gather.6.cloned.1.call-update
  112.9 0.0 all-gather.8.cloned.1.call-start
  112.9 0.5 all-gather.8.cloned.1.call-update
  113.4 11.5 %reduce-scatter.5.cloned.1.call-done = bf16[16,64,1024]{2,1,0:T(8,128)(2,1)} async-done(((bf16[16,64,2048]{2,1,0:T(8,128)(2,1)}), bf16[16,64,1024]{2,1,0:T(8,128)(2,1)}) %reduce-scatter.5.cloned.1.call-update) | async-done | bytes 2097168 | tf_op jit(solution)/shard_map/reduce_scatter | solution.py:63
  124.9 7.0 %all-to-all-start.1 = ((bf16[16,64,1024]{2,1,0:T(8,128)(2,1)}), bf16[16,64,1024]{2,1,0:T(8,128)(2,1)}, u32[]{:S(2)}, u32[]{:S(2)}) async-start(bf16[16,64,1024]{2,1,0:T(8,128)(2,1)} %reduce-scatter.5.cloned.1.call-done), calls=%async_computation.3 | async-start | bytes 4194304 | tf_op jit(solution)/shard_map/all_to_all | solution.py:67
  131.9 0.2 reduce-scatter.3.cloned.1.call-start
  132.1 100.1 %all-gather.12.cloned.1.call-done = bf16[22528,128]{1,0:T(8,128)(2,1)} async-done(((bf16[1408,128]{1,0:T(8,128)(2,1)}), bf16[22528,128]{1,0:T(8,128)(2,1)}) %all-gather.12.cloned.1.call-update) | async-done | bytes 5767184 | tf_op jit(solution)/shard_map/all_gather | solution.py:8
  232.2 8.3 %copy.16 = bf16[1408,16,128]{0,2,1:T(8,128)(2,1)} copy(bf16[1408,16,128]{2,0,1:T(8,128)(2,1)} %bitcast.49) | data formatting | bytes 11534336 | tf_op jit(solution)/shard_map/reshape | solution.py:9
  240.5 81.8 %all-gather.6.cloned.1.call-done = bf16[2048,1408]{1,0:T(8,128)(2,1)} async-done(((bf16[128,1408]{1,0:T(8,128)(2,1)}), bf16[2048,1408]{1,0:T(8,128)(2,1)}) %all-gather.6.cloned.1.call-update) | async-done | bytes 5767184 | tf_op jit(solution)/shard_map/all_gather | solution.py:74
  322.2 4.5 %fusion.24 = f32[128,1408]{1,0:T(8,128)} fusion(bf16[128,2048]{1,0:T(8,128)(2,1)S(1)} %copy-done.1, bf16[2048,1408]{1,0:T(8,128)(2,1)} %all-gather.6.cloned.1.call-done), kind=kOutput, calls=%fused_computation.43 | convolution fusion | flops 738197504 | bytes 7012352 | tf_op jit(solution)/shard_map/dot_general | solution.py:72
  326.7 85.3 %all-gather.8.cloned.1.call-done = bf16[2048,1408]{1,0:T(8,128)(2,1)} async-done(((bf16[128,1408]{1,0:T(8,128)(2,1)}), bf16[2048,1408]{1,0:T(8,128)(2,1)}) %all-gather.8.cloned.1.call-update) | async-done | bytes 5767184 | tf_op jit(solution)/shard_map/all_gather | solution.py:79
  412.1 8.4 %fusion.10 = f32[128,2048]{1,0:T(8,128)} fusion(bf16[1408,2048]{0,1:T(8,128)(2,1)} %bitcast.50, bf16[128,2048]{1,0:T(8,128)(2,1)S(1)} %copy-done.1, bf16[2048,1408]{1,0:T(8,128)(2,1)} %all-gather.8.cloned.1.call-done, f32[128,1408]{1,0:T(8,128)} %fusion.24), kind=kOutput, calls=%fused_computation.14 | convolution fusion | flops 1477476352 | bytes 13828096 | tf_op jit(solution)/shard_map/dot_general | solution.py:83
  420.5 0.0 reduce-scatter.3.cloned.1.call-update
  420.5 0.1 copy.17
  420.6 0.0 all-to-all-done.1
  420.7 6.4 %gather_fusion.1 = bf16[768,1024]{1,0:T(8,128)(2,1)} fusion(bf16[1024,1024]{1,0:T(8,128)(2,1)} %bitcast.10, s32[1024]{0:T(1024)S(1)} %pad_clamp_fusion), kind=kCustom, calls=%fused_computation.1 | custom fusion | bytes 3148800 | tf_op jit(solution)/shard_map/gather | solution.py:69
  427.1 3.9 reshape.86
  431.0 3.6 multiply_reduce_fusion
  434.6 0.0 reduce-scatter.3.cloned.1.call-done
  434.6 1.8 add_convert_fusion
  (10 shorter events, 0.1 us)
Async XLA Ops:
  7.4 93.0 %copy-start = (bf16[1,704,2048]{2,1,0:T(8,128)(2,1)S(1)}, bf16[1,704,2048]{2,1,0:T(8,128)(2,1)}, u32[]{:S(2)}) copy-start(bf16[1,704,2048]{2,1,0:T(8,128)(2,1)} %param.17) | copy-start | bytes 8650756
  7.4 7.9 %copy-start.1 = (bf16[128,2048]{1,0:T(8,128)(2,1)S(1)}, bf16[128,2048]{1,0:T(8,128)(2,1)}, u32[]{:S(2)}) copy-start(bf16[128,2048]{1,0:T(8,128)(2,1)} %param.9) | copy-start | bytes 1572868
  7.4 85.1 %all-gather.10.cloned.1.call-start = ((), (), s32[]{:S(2)}) async-start(), calls=%async_computation.7 | async-start | bytes 6291456 | tf_op jit(solution)/shard_map/all_gather | solution.py:60
  80.4 44.5 %reduce-scatter.5.cloned.1.call-start = ((), (), s32[]{:S(2)}) async-start(), calls=%async_computation.8 | async-start | bytes 6291456 | tf_op jit(solution)/shard_map/reduce_scatter | solution.py:63
  111.7 120.5 %all-gather.12.cloned.1.call-start = ((), (), s32[]{:S(2)}) async-start(), calls=%async_computation.9 | async-start | bytes 6127616 | tf_op jit(solution)/shard_map/all_gather | solution.py:8
  112.3 210.0 %all-gather.6.cloned.1.call-start = ((), (), s32[]{:S(2)}) async-start(), calls=%async_computation.4 | async-start | bytes 6127616 | tf_op jit(solution)/shard_map/all_gather | solution.py:74
  112.9 299.2 %all-gather.8.cloned.1.call-start = ((), (), s32[]{:S(2)}) async-start(), calls=%async_computation.5 | async-start | bytes 6127616 | tf_op jit(solution)/shard_map/all_gather | solution.py:79
  124.9 295.7 %all-to-all-start.1 = ((bf16[16,64,1024]{2,1,0:T(8,128)(2,1)}), bf16[16,64,1024]{2,1,0:T(8,128)(2,1)}, u32[]{:S(2)}, u32[]{:S(2)}) async-start(bf16[16,64,1024]{2,1,0:T(8,128)(2,1)} %reduce-scatter.5.cloned.1.call-done), calls=%async_computation.3 | async-start | bytes 4194304 | tf_op jit(solution)/shard_map/all_to_all | solution.py:67
  131.9 302.7 %reduce-scatter.3.cloned.1.call-start = ((), (), s32[]{:S(2)}) async-start(), calls=%async_computation.6 | async-start | bytes 1572864 | tf_op jit(solution)/shard_map/reduce_scatter | solution.py:86
  412.1 8.4 %copy-start.2 = (f32[128,6]{0,1:T(8,128)S(1)}, f32[128,6]{0,1:T(8,128)}, u32[]{:S(2)}) copy-start(f32[128,6]{0,1:T(8,128)} %param.11) | copy-start | bytes 9220
Sparse Core Ops, SparseCore 0:
  80.5 11.9 all-gather.9
  111.8 13.0 reduce-scatter.4
  420.6 7.1 reduce-scatter.2
Sparse Core Ops, SparseCore 1:
  114.9 117.3 all-gather.11
  234.8 87.4 all-gather.5
  324.8 87.2 all-gather.7
